TPU v7x, 32 devices: a whole 2x2x4 slice. The times are simulated.
32 devices in a mesh: lat: 4 (over x, core), lon: 8 (over z, y).
Axes of the slice: x: 2, y: 2, z: 4, core: 2. Of those that a mesh axis runs over, the one named last changes fastest.
Arguments:
- tracers: bfloat16 [256, 1024, 32, 4], P('lat', 'lon'), may hold values from 0 to 2
- weights: bfloat16 [256, 8, 8, 128, 128], P('lat', 'lon'), may hold values from -1 to 1, as said below
- source_row: int32 [256, 8, 8], P('lat', 'lon'), may hold values from 0 to 255, as said below
- source_block: int32 [256, 8, 8], P('lat', 'lon'), may hold values from 0 to 7, as said below
- slot_count: int32 [256, 8], P('lat', 'lon'), may hold values from 1 to 8, as said below
Outputs:
- advected_fixed: float32 [256, 1024, 32, 4], P('lat', 'lon')
Inputs may be any that keep to these rules, and one draw needn't show every extreme that they name: source_row differs from the target tile's own row by at most 4 and lies within the grid. source_block lies at cyclic distance at most 2 from the target tile's own index along the row, except for target tiles of the first and the last latitude row, where it may reach 3; the allowed distance grows from 1 at the equator towards the poles; in the two outermost rows slot 0 reaches exactly 3 sectors ahead on even tiles and 3 sectors behind on odd tiles. slot_count grows from 1 or 2 at the equator to 8 at the two outermost rows. weights are of either sign; for each target tile the weights of each target cell over the used slots and all source cells sum (before rounding to bfloat16) to one value of that tile between 0.9 and 1.05.
All inputs are finite; a program needn't handle non-finite values.
Results may differ from a plain program's by a relative error of at most 0.0003.
Values may be sent and summed in bfloat16 or wider, within the bound.
A program may use at most 192 MiB of HBM per device.

v0:
```python
import math
import jax
import jax.numpy as jnp
from jax import lax
from jax.sharding import PartitionSpec as P

RLAT = 4
REACH = 3


def extended(value, sides, width):
    for axis, dim in sides:
        size, length = (lax.axis_size(axis), value.shape[dim])
        up = [(i, (i + 1) % size) for i in range(size - 1)]
        down = [(j, i) for i, j in up]
        last = lax.slice_in_dim(value, length - width, length, axis=dim)
        leading = lax.slice_in_dim(value, 0, width, axis=dim)
        before = lax.ppermute(last, axis, up)
        after = lax.ppermute(leading, axis, down)
        value = jnp.concatenate([before, value, after], axis=dim)
    return value


def shifted(value, axis, by):
    length = lax.axis_size(axis)
    return lax.ppermute(value, axis, [(i, (i + by) % length) for i in range(length)])


def latitude_area(total_rows, first_row, count_rows):
    rows_all = jnp.arange(count_rows, dtype=jnp.int32) + first_row
    angle = -0.5 * math.pi + (rows_all.astype(jnp.float32) + 0.5) * (math.pi / total_rows)
    return jnp.cos(angle)


def local(tracers, weights, source_row, source_block, slot_count):
    rows_dev, tile_width, levels, tracer_kinds = tracers.shape
    channels = levels * tracer_kinds
    lat_count = lax.axis_size("lat")
    lon_count = lax.axis_size("lon")
    lat_index = lax.axis_index("lat")
    lon_index = lax.axis_index("lon")
    field = tracers.reshape(rows_dev, tile_width, channels)
    total_rows = rows_dev * lat_count
    area = latitude_area(total_rows, lat_index * rows_dev, rows_dev)
    total_area = tile_width * lon_count * jnp.sum(latitude_area(total_rows, 0, total_rows))
    mass_old = jnp.sum(area[:, None, None] * field, axis=(0, 1))
    padded = extended(field, (("lat", 0),), RLAT)
    local_row = source_row[:, 0, :] - (lat_index * rows_dev - RLAT)
    wanted = source_block[:, 0, :]
    slots_max = source_row.shape[2]
    relative = (wanted - lon_index + REACH) % lon_count - REACH
    near_list = []
    for distance in range(-(REACH - 1), REACH):
        if distance == 0:
            near_list.append(padded)
        else:
            near_list.append(shifted(padded, "lon", -distance))
    near_stack = jnp.stack(near_list, axis=1)
    near_pick = near_stack[local_row, jnp.clip(relative + REACH - 1, 0, 2 * REACH - 2)]
    polar_slab = jnp.concatenate(
        [padded[RLAT : 2 * RLAT + 1], padded[rows_dev - 1 : rows_dev + RLAT]], axis=0
    )
    far_list = [shifted(polar_slab, "lon", -distance) for distance in (-REACH, REACH)]
    upper = (jnp.arange(rows_dev, dtype=jnp.int32) < rows_dev // 2)[:, None]
    far_row = jnp.where(upper, local_row - RLAT, local_row - (rows_dev - 1) + RLAT + 1)
    far_row = jnp.clip(far_row, 0, 2 * RLAT + 1)
    far_stack = jnp.stack(far_list, axis=1)
    far_pick = far_stack[
        jnp.clip(far_row, 0, far_stack.shape[0] - 1), (relative > 0).astype(jnp.int32)
    ]
    active = jnp.arange(slots_max, dtype=jnp.int32)[None, :] < slot_count
    is_far = jnp.abs(relative) == REACH
    picked = jnp.where(
        (active & is_far)[:, :, None, None],
        far_pick,
        jnp.where(active[:, :, None, None], near_pick, jnp.zeros((), near_pick.dtype)),
    )
    advected = jnp.einsum(
        "tkij,tkjc->tic", weights[:, 0], picked, preferred_element_type=jnp.float32
    )
    mass_new = jnp.sum(area[:, None, None] * advected, axis=(0, 1))
    summed_old, summed_new = lax.psum((mass_old, mass_new), ("lat", "lon"))
    fixed = advected + (summed_old - summed_new) / total_area
    return fixed.reshape(rows_dev, tile_width, levels, tracer_kinds)


def solution(mesh):
    return jax.shard_map(
        local,
        mesh=mesh,
        in_specs=(
            P("lat", "lon", None, None),
            P("lat", "lon", None, None, None),
            P("lat", "lon", None),
            P("lat", "lon", None),
            P("lat", "lon"),
        ),
        out_specs=P("lat", "lon", None, None),
        check_vma=False,
    )
```

profile of v0, /device:TPU:10, one launch (start us, length us, event | category | flops | bytes accessed | tf_op | source)
XLA Modules:
  0.0 299.7 jit_solution(15914645323149280018)
XLA Ops:
  0.0 1.2 fusion.28
  1.2 1.9 collective-permute-start.2
  3.2 3.6 %collective-permute-start.3 = (bf16[4,128,128]{1,2,0:T(8,128)(2,1)S(1)}, bf16[4,128,128]{1,2,0:T(8,128)(2,1)S(1)}, u32[]{:S(2)}, u32[]{:S(2)}) collective-permute-start(bf16[4,128,128]{1,2,0:T(8,128)(2,1)S(1)} %bitcast.72), channel_id=1, source_target_pairs={{8,0},{16,8},{24,16},{9,1},{17,9},{25,17},{10,2},{18,10},{26,18},{... | collective-permute-start | bytes 393224 | tf_op jit(solution)/shard_map/ppermute | solution.py:19
  7.5 1.8 collective-permute-done.3
  9.3 3.3 %pad_maximum_fusion = bf16[72,128,128]{1,2,0:T(8,128)(2,1)} fusion(bf16[4,128,128]{1,2,0:T(8,128)(2,1)S(1)} %collective-permute-done.3, bf16[64,128,128]{1,2,0:T(8,128)(2,1)} %bitcast.64, bf16[4,128,128]{1,2,0:T(8,128)(2,1)S(1)} %collective-permute-done.2), kind=kLoop, calls=%fused_computation.13 | loop fusion | flops 2359296 | bytes 4718592 | tf_op jit(solution)/shard_map/concatenate | solution.py:20
  12.6 1.6 collective-permute-start.4
  14.2 1.5 collective-permute-start.5
  15.7 1.4 collective-permute-start.6
  17.2 2.3 collective-permute-start.7
  19.7 153.8 %collective-permute-done = bf16[10,128,128]{1,2,0:T(8,128)(2,1)S(1)} collective-permute-done((bf16[10,128,128]{1,2,0:T(8,128)(2,1)S(1)}, bf16[10,128,128]{1,2,0:T(8,128)(2,1)S(1)}, u32[]{:S(2)}, u32[]{:S(2)}) %collective-permute-start) | collective-permute-done | bytes 327712 | tf_op jit(solution)/shard_map/ppermute | solution.py:26
  173.5 1.3 collective-permute-start.1
  175.4 1.4 multiply_reduce_fusion
  178.1 9.5 %collective-permute-done.1 = bf16[10,128,128]{1,2,0:T(8,128)(2,1)S(1)} collective-permute-done((bf16[10,128,128]{1,2,0:T(8,128)(2,1)S(1)}, bf16[10,128,128]{1,2,0:T(8,128)(2,1)S(1)}, u32[]{:S(2)}, u32[]{:S(2)}) %collective-permute-start.1) | collective-permute-done | bytes 327712 | tf_op jit(solution)/shard_map/ppermute | solution.py:26
  188.3 1.0 pad_maximum_fusion.1
  189.4 10.8 %gather_fusion = bf16[512,128,128]{1,2,0:T(8,128)(2,1)} fusion(bf16[10,2,128,128]{2,3,0,1:T(8,128)(2,1)S(1)} %pad_maximum_fusion.1, s32[512]{0:T(512)S(1)} %reshape.252), kind=kCustom, calls=%fused_computation | custom fusion | bytes 33558528 | tf_op jit(solution)/shard_map/gather | solution.py:68
  200.2 3.3 %bitcast_dynamic-update-slice_fusion.4 = bf16[72,5,128,128]{2,3,0,1:T(8,128)(2,1)} fusion(bf16[72,128,128]{1,2,0:T(8,128)(2,1)} %collective-permute-done.4), kind=kLoop, calls=%fused_computation.18 | loop fusion | bytes 4718592
  203.5 3.4 %bitcast_dynamic-update-slice_fusion.3 = bf16[72,5,128,128]{2,3,0,1:T(8,128)(2,1)} fusion(bf16[72,5,128,128]{2,3,0,1:T(8,128)(2,1)} %bitcast_dynamic-update-slice_fusion.4, bf16[72,128,128]{1,2,0:T(8,128)(2,1)} %collective-permute-done.5), kind=kLoop, calls=%fused_computation.17 | loop fusion | bytes 4718592
  206.9 1.7 bitcast_dynamic-update-slice_fusion.2
  208.6 3.4 %bitcast_dynamic-update-slice_fusion.1 = bf16[72,5,128,128]{2,3,0,1:T(8,128)(2,1)} fusion(bf16[72,5,128,128]{2,3,0,1:T(8,128)(2,1)} %bitcast_dynamic-update-slice_fusion.2, bf16[72,128,128]{1,2,0:T(8,128)(2,1)} %collective-permute-done.6), kind=kLoop, calls=%fused_computation.15 | loop fusion | bytes 4718592
  212.0 3.4 %bitcast_dynamic-update-slice_fusion = bf16[72,5,128,128]{2,3,0,1:T(8,128)(2,1)} fusion(bf16[72,5,128,128]{2,3,0,1:T(8,128)(2,1)} %bitcast_dynamic-update-slice_fusion.1, bf16[72,128,128]{1,2,0:T(8,128)(2,1)} %collective-permute-done.7), kind=kLoop, calls=%fused_computation.14 | loop fusion | bytes 4718592 | tf_op jit(solution)/shard_map/stack | solution.py:58
  215.4 15.2 %gather_fusion.1 = bf16[512,128,128]{1,2,0:T(8,128)(2,1)} fusion(bf16[72,5,128,128]{2,3,0,1:T(8,128)(2,1)} %bitcast_dynamic-update-slice_fusion, s32[512]{0:T(512)S(1)} %reshape.258), kind=kCustom, calls=%fused_computation.1 | custom fusion | bytes 33558528 | tf_op jit(solution)/shard_map/gather | solution.py:59
  230.5 19.4 %fusion.7 = (f32[128]{0:T(128)S(1)}, f32[64,128,128,1]{2,1,3,0:T(8,128)}) fusion(f32[64]{0:T(128)S(1)} %add_cosine_fusion, bf16[64,1,8,128,128]{4,3,2,1,0:T(8,128)(2,1)} %param.6, bf16[64,8,128,128]{2,3,1,0:T(8,128)(2,1)} %bitcast.66, bf16[64,8,128,128]{2,3,1,0:T(8,128)(2,1)} %bitcast.67, pred[64,8]{1,0:T(8,128)(4,1)S(1)} %copy.10, pred[64,8]{1,0:T(8,128)(4,1)S(1)} %copy.8), kind=kOutput, calls=%fused_computation.11 | convolution fusion | flops 2166358016 | bytes 54527744 | tf_op jit(solution)/shard_map/tkij,tkjc->tic/dot_general | solution.py:78
  250.0 44.8 %all-reduce = (f32[128]{0:T(128)S(1)}, f32[128]{0:T(128)S(1)}) all-reduce(f32[128]{0:T(128)S(1)} %reduce_sum.30, f32[128]{0:T(128)S(1)} %get-tuple-element.15), channel_id=1, replica_groups=mesh['lat'=4,'lon'=8] {'lat','lon'}, use_global_device_ids=true, to_apply=%region_1.0 | all-reduce | flops 256 | bytes 2048 | tf_op jit(solution)/shard_map/psum | solution.py:82
  294.8 4.9 %bitcast_add_fusion = f32[64,128,128]{2,1,0:T(8,128)} fusion(f32[64,128,128,1]{2,1,3,0:T(8,128)} %get-tuple-element.16, f32[128]{0:T(128)S(1)} %subtract_divide_fusion), kind=kLoop, calls=%fused_computation.9 | loop fusion | flops 1048576 | bytes 8389120 | tf_op jit(solution)/shard_map/add | solution.py:83
  (31 shorter events, 3.1 us)
Async XLA Ops:
  0.0 17.1 %copy-start = (bf16[64,128,32,4]{1,3,2,0:T(4,128)(2,1)S(1)}, bf16[64,128,32,4]{1,3,2,0:T(4,128)(2,1)}, u32[]{:S(2)}) copy-start(bf16[64,128,32,4]{1,3,2,0:T(4,128)(2,1)} %param.5) | copy-start | bytes 6291460
  0.0 19.6 %copy-start.2 = (s32[64,1,8]{0,2,1:T(8,128)S(1)}, s32[64,1,8]{0,2,1:T(8,128)}, u32[]{:S(2)}) copy-start(s32[64,1,8]{0,2,1:T(8,128)} %param.8) | copy-start | bytes 6148
  0.0 19.7 %copy-start.4 = (s32[64,1]{0,1:T(1,128)S(1)}, s32[64,1]{0,1:T(1,128)}, u32[]{:S(2)}) copy-start(s32[64,1]{0,1:T(1,128)} %param.9) | copy-start | bytes 772
  0.0 19.7 %copy-start.3 = (s32[64,1,8]{0,2,1:T(8,128)S(1)}, s32[64,1,8]{0,2,1:T(8,128)}, u32[]{:S(2)}) copy-start(s32[64,1,8]{0,2,1:T(8,128)} %param.7) | copy-start | bytes 6148
  1.2 6.3 %collective-permute-start.2 = (bf16[4,128,128]{1,2,0:T(8,128)(2,1)S(1)}, bf16[4,128,128]{1,2,0:T(8,128)(2,1)S(1)}, u32[]{:S(2)}, u32[]{:S(2)}) collective-permute-start(bf16[4,128,128]{1,2,0:T(8,128)(2,1)S(1)} %bitcast.73), channel_id=1, source_target_pairs={{0,8},{8,16},{16,24},{1,9},{9,17},{17,25},{2,10},{10,18},{18,26},{... | collective-permute-start | bytes 393224 | tf_op jit(solution)/shard_map/ppermute | solution.py:18
  3.2 6.1 %collective-permute-start.3 = (bf16[4,128,128]{1,2,0:T(8,128)(2,1)S(1)}, bf16[4,128,128]{1,2,0:T(8,128)(2,1)S(1)}, u32[]{:S(2)}, u32[]{:S(2)}) collective-permute-start(bf16[4,128,128]{1,2,0:T(8,128)(2,1)S(1)} %bitcast.72), channel_id=1, source_target_pairs={{8,0},{16,8},{24,16},{9,1},{17,9},{25,17},{10,2},{18,10},{26,18},{... | collective-permute-start | bytes 393224 | tf_op jit(solution)/shard_map/ppermute | solution.py:19
  12.6 187.6 %collective-permute-start.4 = (bf16[72,128,128]{1,2,0:T(8,128)(2,1)}, bf16[72,128,128]{1,2,0:T(8,128)(2,1)}, u32[]{:S(2)}, u32[]{:S(2)}) collective-permute-start(bf16[72,128,128]{1,2,0:T(8,128)(2,1)} %pad_maximum_fusion), channel_id=1, source_target_pairs={{0,2},{1,3},{2,4},{3,5},{4,6},{5,7},{6,0},{7,1},{8,10},{9,11},{10,... | collective-permute-start | bytes 7077896 | tf_op jit(solution)/shard_map/ppermute | solution.py:26
  14.2 189.3 %collective-permute-start.5 = (bf16[72,128,128]{1,2,0:T(8,128)(2,1)}, bf16[72,128,128]{1,2,0:T(8,128)(2,1)}, u32[]{:S(2)}, u32[]{:S(2)}) collective-permute-start(bf16[72,128,128]{1,2,0:T(8,128)(2,1)} %pad_maximum_fusion), channel_id=1, source_target_pairs={{0,1},{1,2},{2,3},{3,4},{4,5},{5,6},{6,7},{7,0},{8,9},{9,10},{10,1... | collective-permute-start | bytes 7077896 | tf_op jit(solution)/shard_map/ppermute | solution.py:26
  15.7 192.9 %collective-permute-start.6 = (bf16[72,128,128]{1,2,0:T(8,128)(2,1)}, bf16[72,128,128]{1,2,0:T(8,128)(2,1)}, u32[]{:S(2)}, u32[]{:S(2)}) collective-permute-start(bf16[72,128,128]{1,2,0:T(8,128)(2,1)} %pad_maximum_fusion), channel_id=1, source_target_pairs={{0,7},{1,0},{2,1},{3,2},{4,3},{5,4},{6,5},{7,6},{8,15},{9,8},{10,9... | collective-permute-start | bytes 7077896 | tf_op jit(solution)/shard_map/ppermute | solution.py:26
  17.2 194.7 %collective-permute-start.7 = (bf16[72,128,128]{1,2,0:T(8,128)(2,1)}, bf16[72,128,128]{1,2,0:T(8,128)(2,1)}, u32[]{:S(2)}, u32[]{:S(2)}) collective-permute-start(bf16[72,128,128]{1,2,0:T(8,128)(2,1)} %pad_maximum_fusion), channel_id=1, source_target_pairs={{0,6},{1,7},{2,0},{3,1},{4,2},{5,3},{6,4},{7,5},{8,14},{9,15},{10,... | collective-permute-start | bytes 7077896 | tf_op jit(solution)/shard_map/ppermute | solution.py:26
  19.6 154.0 %collective-permute-start = (bf16[10,128,128]{1,2,0:T(8,128)(2,1)S(1)}, bf16[10,128,128]{1,2,0:T(8,128)(2,1)S(1)}, u32[]{:S(2)}, u32[]{:S(2)}) collective-permute-start(bf16[10,128,128]{1,2,0:T(8,128)(2,1)S(1)} %pad_maximum_fusion.2), channel_id=1, source_target_pairs={{0,3},{1,4},{2,5},{3,6},{4,7},{5,0},{6,1},{7,2},{8,11},{9,12},{10,... | collective-permute-start | bytes 983048 | tf_op jit(solution)/shard_map/ppermute | solution.py:26
  173.5 14.1 %collective-permute-start.1 = (bf16[10,128,128]{1,2,0:T(8,128)(2,1)S(1)}, bf16[10,128,128]{1,2,0:T(8,128)(2,1)S(1)}, u32[]{:S(2)}, u32[]{:S(2)}) collective-permute-start(bf16[10,128,128]{1,2,0:T(8,128)(2,1)S(1)} %pad_maximum_fusion.2), channel_id=1, source_target_pairs={{0,5},{1,6},{2,7},{3,0},{4,1},{5,2},{6,3},{7,4},{8,13},{9,14},{10,... | collective-permute-start | bytes 983048 | tf_op jit(solution)/shard_map/ppermute | solution.py:26
  187.6 0.7 copy-start.1
where the time goes:
time: 300 us
  waiting for transfers between devices  166 us (55%)
  blocking collectives  44.8 us (15%)
  local copies, waits for them, and re-layouts  42.2 us (14%)
  matrix products  19.4 us (6%)
  starting transfers between devices  13.7 us (5%)
  other arithmetic  13.1 us (4%)
    ppermute x6, waiting for transfers between devices, shifted(): lax.ppermute(value, axis, [(i, (i + by) % length) for i in range(length)])  163 us
    psum x1, blocking collectives, local(): summed_old, summed_new = lax.psum((mass_old, mass_new), ('lat', 'lon'))  44.8 us
    dot_general x1, matrix products, local(): jnp.einsum('tkij,tkjc->tic', weights[:, 0], picked, preferred_element_typ...  19.4 us
    gather x1, local copies, waits for them, and re-layouts, local(): near_stack[local_row, jnp.clip(relative + REACH - 1, 0, 2 * REACH - 2)]  15.2 us
    unnamed x13, local copies, waits for them, and re-layouts  10.8 us
    gather x1, local copies, waits for them, and re-layouts, local(): far_stack[jnp.clip(far_row, 0, far_stack.shape[0] - 1), (relative > 0).as...  10.8 us
    ppermute x6, starting transfers between devices, shifted(): lax.ppermute(value, axis, [(i, (i + by) % length) for i in range(length)])  8.16 us
  transfers between devices with their start and end apart: 8, of which 4 were waited for; matrix products, arithmetic and copies ran while one was open for 9% of the time, Pallas kernels for 0%

commit v1 on v0

--- a/solution.py
+++ b/solution.py
@@ -79,7 +79,8 @@
         "tkij,tkjc->tic", weights[:, 0], picked, preferred_element_type=jnp.float32
     )
     mass_new = jnp.sum(area[:, None, None] * advected, axis=(0, 1))
-    summed_old, summed_new = lax.psum((mass_old, mass_new), ("lat", "lon"))
+    show_halves = lambda row_data: lax.psum(lax.psum(row_data, "lon"), "lat")
+    summed_old, summed_new = show_halves((mass_old, mass_new))
     fixed = advected + (summed_old - summed_new) / total_area
     return fixed.reshape(rows_dev, tile_width, levels, tracer_kinds)
 

time: 300 us -> 286 us (0.953)
  the two profiles are of different devices: /device:TPU:10 before, /device:TPU:0 now
where the time goes in v1:
time: 286 us; the launch traced here: 285 us
  waiting for transfers between devices  176 us (62%)
  local copies, waits for them, and re-layouts  42.2 us (15%)
  blocking collectives  22.9 us (8%)
  matrix products  19.4 us (7%)
  other arithmetic  13.1 us (5%)
  starting transfers between devices  10.6 us (4%)
    ppermute x6, waiting for transfers between devices, shifted(): lax.ppermute(value, axis, [(i, (i + by) % length) for i in range(length)])  172 us
    psum x2, blocking collectives, local(): show_halves = lambda row_data: lax.psum(lax.psum(row_data, 'lon'), 'lat')  22.9 us
    dot_general x1, matrix products, local(): jnp.einsum('tkij,tkjc->tic', weights[:, 0], picked, preferred_element_typ...  19.4 us
    gather x1, local copies, waits for them, and re-layouts, local(): near_stack[local_row, jnp.clip(relative + REACH - 1, 0, 2 * REACH - 2)]  15.2 us
    unnamed x13, local copies, waits for them, and re-layouts  10.8 us
    gather x1, local copies, waits for them, and re-layouts, local(): far_stack[jnp.clip(far_row, 0, far_stack.shape[0] - 1), (relative > 0).as...  10.8 us
    ppermute x6, starting transfers between devices, shifted(): lax.ppermute(value, axis, [(i, (i + by) % length) for i in range(length)])  6.86 us
  transfers between devices with their start and end apart: 8, of which 3 were waited for; matrix products, arithmetic and copies ran while one was open for 9% of the time, Pallas kernels for 0%

profile of v1, /device:TPU:0, one launch (start us, length us, event | category | flops | bytes accessed | tf_op | source)
XLA Modules:
  0.0 285.1 jit_solution(1484090268252561327)
XLA Ops:
  0.0 1.2 fusion.28
  1.2 2.4 collective-permute-start.2
  3.6 1.3 collective-permute-start.3
  5.0 4.0 %collective-permute-done.3 = bf16[4,128,128]{1,2,0:T(8,128)(2,1)S(1)} collective-permute-done((bf16[4,128,128]{1,2,0:T(8,128)(2,1)S(1)}, bf16[4,128,128]{1,2,0:T(8,128)(2,1)S(1)}, u32[]{:S(2)}, u32[]{:S(2)}) %collective-permute-start.3) | collective-permute-done | bytes 131104 | tf_op jit(solution)/shard_map/ppermute | solution.py:19
  9.0 3.3 %pad_maximum_fusion = bf16[72,128,128]{1,2,0:T(8,128)(2,1)} fusion(bf16[4,128,128]{1,2,0:T(8,128)(2,1)S(1)} %collective-permute-done.3, bf16[64,128,128]{1,2,0:T(8,128)(2,1)} %bitcast.64, bf16[4,128,128]{1,2,0:T(8,128)(2,1)S(1)} %collective-permute-done.2), kind=kLoop, calls=%fused_computation.13 | loop fusion | flops 2359296 | bytes 4718592 | tf_op jit(solution)/shard_map/concatenate | solution.py:20
  12.3 1.6 collective-permute-start.4
  13.8 1.5 collective-permute-start.5
  15.4 3.2 %collective-permute-start.6 = (bf16[72,128,128]{1,2,0:T(8,128)(2,1)}, bf16[72,128,128]{1,2,0:T(8,128)(2,1)}, u32[]{:S(2)}, u32[]{:S(2)}) collective-permute-start(bf16[72,128,128]{1,2,0:T(8,128)(2,1)} %pad_maximum_fusion), channel_id=1, source_target_pairs={{0,7},{1,0},{2,1},{3,2},{4,3},{5,4},{6,5},{7,6},{8,15},{9,8},{10,9... | collective-permute-start | bytes 7077896 | tf_op jit(solution)/shard_map/ppermute | solution.py:26
  19.4 165.0 %collective-permute-done = bf16[10,128,128]{1,2,0:T(8,128)(2,1)S(1)} collective-permute-done((bf16[10,128,128]{1,2,0:T(8,128)(2,1)S(1)}, bf16[10,128,128]{1,2,0:T(8,128)(2,1)S(1)}, u32[]{:S(2)}, u32[]{:S(2)}) %collective-permute-start) | collective-permute-done | bytes 327712 | tf_op jit(solution)/shard_map/ppermute | solution.py:26
  185.0 1.4 multiply_reduce_fusion
  187.7 7.3 %collective-permute-done.1 = bf16[10,128,128]{1,2,0:T(8,128)(2,1)S(1)} collective-permute-done((bf16[10,128,128]{1,2,0:T(8,128)(2,1)S(1)}, bf16[10,128,128]{1,2,0:T(8,128)(2,1)S(1)}, u32[]{:S(2)}, u32[]{:S(2)}) %collective-permute-start.1) | collective-permute-done | bytes 327712 | tf_op jit(solution)/shard_map/ppermute | solution.py:26
  195.1 0.7 copy-done.1
  195.8 1.0 pad_maximum_fusion.1
  196.8 10.8 %gather_fusion = bf16[512,128,128]{1,2,0:T(8,128)(2,1)} fusion(bf16[10,2,128,128]{2,3,0,1:T(8,128)(2,1)S(1)} %pad_maximum_fusion.1, s32[512]{0:T(512)S(1)} %reshape.252), kind=kCustom, calls=%fused_computation | custom fusion | bytes 33558528 | tf_op jit(solution)/shard_map/gather | solution.py:68
  207.6 3.3 %bitcast_dynamic-update-slice_fusion.4 = bf16[72,5,128,128]{2,3,0,1:T(8,128)(2,1)} fusion(bf16[72,128,128]{1,2,0:T(8,128)(2,1)} %collective-permute-done.4), kind=kLoop, calls=%fused_computation.18 | loop fusion | bytes 4718592
  210.9 3.4 %bitcast_dynamic-update-slice_fusion.3 = bf16[72,5,128,128]{2,3,0,1:T(8,128)(2,1)} fusion(bf16[72,5,128,128]{2,3,0,1:T(8,128)(2,1)} %bitcast_dynamic-update-slice_fusion.4, bf16[72,128,128]{1,2,0:T(8,128)(2,1)} %collective-permute-done.5), kind=kLoop, calls=%fused_computation.17 | loop fusion | bytes 4718592
  214.3 1.7 bitcast_dynamic-update-slice_fusion.2
  216.0 3.4 %bitcast_dynamic-update-slice_fusion.1 = bf16[72,5,128,128]{2,3,0,1:T(8,128)(2,1)} fusion(bf16[72,5,128,128]{2,3,0,1:T(8,128)(2,1)} %bitcast_dynamic-update-slice_fusion.2, bf16[72,128,128]{1,2,0:T(8,128)(2,1)} %collective-permute-done.6), kind=kLoop, calls=%fused_computation.15 | loop fusion | bytes 4718592
  219.4 3.4 %bitcast_dynamic-update-slice_fusion = bf16[72,5,128,128]{2,3,0,1:T(8,128)(2,1)} fusion(bf16[72,5,128,128]{2,3,0,1:T(8,128)(2,1)} %bitcast_dynamic-update-slice_fusion.1, bf16[72,128,128]{1,2,0:T(8,128)(2,1)} %collective-permute-done.7), kind=kLoop, calls=%fused_computation.14 | loop fusion | bytes 4718592 | tf_op jit(solution)/shard_map/stack | solution.py:58
  222.8 15.2 %gather_fusion.1 = bf16[512,128,128]{1,2,0:T(8,128)(2,1)} fusion(bf16[72,5,128,128]{2,3,0,1:T(8,128)(2,1)} %bitcast_dynamic-update-slice_fusion, s32[512]{0:T(512)S(1)} %reshape.258), kind=kCustom, calls=%fused_computation.1 | custom fusion | bytes 33558528 | tf_op jit(solution)/shard_map/gather | solution.py:59
  237.9 19.4 %fusion.7 = (f32[128]{0:T(128)S(1)}, f32[64,128,128,1]{2,1,3,0:T(8,128)}) fusion(f32[64]{0:T(128)S(1)} %add_cosine_fusion, bf16[64,1,8,128,128]{4,3,2,1,0:T(8,128)(2,1)} %param.6, bf16[64,8,128,128]{2,3,1,0:T(8,128)(2,1)} %bitcast.66, bf16[64,8,128,128]{2,3,1,0:T(8,128)(2,1)} %bitcast.67, pred[64,8]{1,0:T(8,128)(4,1)S(1)} %copy.10, pred[64,8]{1,0:T(8,128)(4,1)S(1)} %copy.8), kind=kOutput, calls=%fused_computation.11 | convolution fusion | flops 2166358016 | bytes 54527744 | tf_op jit(solution)/shard_map/tkij,tkjc->tic/dot_general | solution.py:78
  257.4 17.1 %all-reduce = (f32[128]{0:T(128)S(1)}, f32[128]{0:T(128)S(1)}) all-reduce(f32[128]{0:T(128)S(1)} %reduce_sum.30, f32[128]{0:T(128)S(1)} %get-tuple-element.17), channel_id=1, replica_groups=mesh['lat'=4,'lon'=8] {'lon'}, use_global_device_ids=true, to_apply=%region_1.0 | all-reduce | flops 256 | bytes 2048 | tf_op jit(solution)/shard_map/psum | solution.py:82
  274.5 5.7 %all-reduce.1 = (f32[128]{0:T(128)S(1)}, f32[128]{0:T(128)S(1)}) all-reduce(f32[128]{0:T(128)S(1)} %get-tuple-element.5, f32[128]{0:T(128)S(1)} %get-tuple-element.6), channel_id=1, replica_groups=mesh['lat'=4,'lon'=8] {'lat'}, use_global_device_ids=true, to_apply=%region_2.3 | all-reduce | flops 256 | bytes 2048 | tf_op jit(solution)/shard_map/psum | solution.py:82
  280.2 4.9 %bitcast_add_fusion = f32[64,128,128]{2,1,0:T(8,128)} fusion(f32[64,128,128,1]{2,1,3,0:T(8,128)} %get-tuple-element.18, f32[128]{0:T(128)S(1)} %subtract_divide_fusion), kind=kLoop, calls=%fused_computation.9 | loop fusion | flops 1048576 | bytes 8389120 | tf_op jit(solution)/shard_map/add | solution.py:84
  (32 shorter events, 2.2 us)
Async XLA Ops:
  0.0 18.6 %copy-start = (bf16[64,128,32,4]{1,3,2,0:T(4,128)(2,1)S(1)}, bf16[64,128,32,4]{1,3,2,0:T(4,128)(2,1)}, u32[]{:S(2)}) copy-start(bf16[64,128,32,4]{1,3,2,0:T(4,128)(2,1)} %param.5) | copy-start | bytes 6291460
  0.0 19.3 %copy-start.2 = (s32[64,1,8]{0,2,1:T(8,128)S(1)}, s32[64,1,8]{0,2,1:T(8,128)}, u32[]{:S(2)}) copy-start(s32[64,1,8]{0,2,1:T(8,128)} %param.8) | copy-start | bytes 6148
  0.0 19.3 %copy-start.4 = (s32[64,1]{0,1:T(1,128)S(1)}, s32[64,1]{0,1:T(1,128)}, u32[]{:S(2)}) copy-start(s32[64,1]{0,1:T(1,128)} %param.9) | copy-start | bytes 772
  0.0 19.4 %copy-start.3 = (s32[64,1,8]{0,2,1:T(8,128)S(1)}, s32[64,1,8]{0,2,1:T(8,128)}, u32[]{:S(2)}) copy-start(s32[64,1,8]{0,2,1:T(8,128)} %param.7) | copy-start | bytes 6148
  1.2 3.7 %collective-permute-start.2 = (bf16[4,128,128]{1,2,0:T(8,128)(2,1)S(1)}, bf16[4,128,128]{1,2,0:T(8,128)(2,1)S(1)}, u32[]{:S(2)}, u32[]{:S(2)}) collective-permute-start(bf16[4,128,128]{1,2,0:T(8,128)(2,1)S(1)} %bitcast.73), channel_id=1, source_target_pairs={{0,8},{8,16},{16,24},{1,9},{9,17},{17,25},{2,10},{10,18},{18,26},{... | collective-permute-start | bytes 393224 | tf_op jit(solution)/shard_map/ppermute | solution.py:18
  3.6 5.3 %collective-permute-start.3 = (bf16[4,128,128]{1,2,0:T(8,128)(2,1)S(1)}, bf16[4,128,128]{1,2,0:T(8,128)(2,1)S(1)}, u32[]{:S(2)}, u32[]{:S(2)}) collective-permute-start(bf16[4,128,128]{1,2,0:T(8,128)(2,1)S(1)} %bitcast.72), channel_id=1, source_target_pairs={{8,0},{16,8},{24,16},{9,1},{17,9},{25,17},{10,2},{18,10},{26,18},{... | collective-permute-start | bytes 393224 | tf_op jit(solution)/shard_map/ppermute | solution.py:19
  12.3 195.3 %collective-permute-start.4 = (bf16[72,128,128]{1,2,0:T(8,128)(2,1)}, bf16[72,128,128]{1,2,0:T(8,128)(2,1)}, u32[]{:S(2)}, u32[]{:S(2)}) collective-permute-start(bf16[72,128,128]{1,2,0:T(8,128)(2,1)} %pad_maximum_fusion), channel_id=1, source_target_pairs={{0,2},{1,3},{2,4},{3,5},{4,6},{5,7},{6,0},{7,1},{8,10},{9,11},{10,... | collective-permute-start | bytes 7077896 | tf_op jit(solution)/shard_map/ppermute | solution.py:26
  13.8 197.1 %collective-permute-start.5 = (bf16[72,128,128]{1,2,0:T(8,128)(2,1)}, bf16[72,128,128]{1,2,0:T(8,128)(2,1)}, u32[]{:S(2)}, u32[]{:S(2)}) collective-permute-start(bf16[72,128,128]{1,2,0:T(8,128)(2,1)} %pad_maximum_fusion), channel_id=1, source_target_pairs={{0,1},{1,2},{2,3},{3,4},{4,5},{5,6},{6,7},{7,0},{8,9},{9,10},{10,1... | collective-permute-start | bytes 7077896 | tf_op jit(solution)/shard_map/ppermute | solution.py:26
  15.4 200.7 %collective-permute-start.6 = (bf16[72,128,128]{1,2,0:T(8,128)(2,1)}, bf16[72,128,128]{1,2,0:T(8,128)(2,1)}, u32[]{:S(2)}, u32[]{:S(2)}) collective-permute-start(bf16[72,128,128]{1,2,0:T(8,128)(2,1)} %pad_maximum_fusion), channel_id=1, source_target_pairs={{0,7},{1,0},{2,1},{3,2},{4,3},{5,4},{6,5},{7,6},{8,15},{9,8},{10,9... | collective-permute-start | bytes 7077896 | tf_op jit(solution)/shard_map/ppermute | solution.py:26
  18.7 200.7 %collective-permute-start.7 = (bf16[72,128,128]{1,2,0:T(8,128)(2,1)}, bf16[72,128,128]{1,2,0:T(8,128)(2,1)}, u32[]{:S(2)}, u32[]{:S(2)}) collective-permute-start(bf16[72,128,128]{1,2,0:T(8,128)(2,1)} %pad_maximum_fusion), channel_id=1, source_target_pairs={{0,6},{1,7},{2,0},{3,1},{4,2},{5,3},{6,4},{7,5},{8,14},{9,15},{10,... | collective-permute-start | bytes 7077896 | tf_op jit(solution)/shard_map/ppermute | solution.py:26
  19.2 165.2 %collective-permute-start = (bf16[10,128,128]{1,2,0:T(8,128)(2,1)S(1)}, bf16[10,128,128]{1,2,0:T(8,128)(2,1)S(1)}, u32[]{:S(2)}, u32[]{:S(2)}) collective-permute-start(bf16[10,128,128]{1,2,0:T(8,128)(2,1)S(1)} %pad_maximum_fusion.2), channel_id=1, source_target_pairs={{0,3},{1,4},{2,5},{3,6},{4,7},{5,0},{6,1},{7,2},{8,11},{9,12},{10,... | collective-permute-start | bytes 983048 | tf_op jit(solution)/shard_map/ppermute | solution.py:26
  184.4 10.6 %collective-permute-start.1 = (bf16[10,128,128]{1,2,0:T(8,128)(2,1)S(1)}, bf16[10,128,128]{1,2,0:T(8,128)(2,1)S(1)}, u32[]{:S(2)}, u32[]{:S(2)}) collective-permute-start(bf16[10,128,128]{1,2,0:T(8,128)(2,1)S(1)} %pad_maximum_fusion.2), channel_id=1, source_target_pairs={{0,5},{1,6},{2,7},{3,0},{4,1},{5,2},{6,3},{7,4},{8,13},{9,14},{10,... | collective-permute-start | bytes 983048 | tf_op jit(solution)/shard_map/ppermute | solution.py:26
  195.0 0.7 copy-start.1
